TPU v7x, 32 devices: a whole 2x2x4 slice. The times are simulated.
32 devices in a mesh: row: 8 (over z, core), col: 4 (over y, x).
Axes of the slice: x: 2, y: 2, z: 4, core: 2. Of those that a mesh axis runs over, the one named last changes fastest.
Arguments:
- factor: bfloat16 [8192, 8192], P('row', 'col'), as said below
- sel_tiles: int32 [32], replicated, may hold values from 0 to 63, as said below
- coupling: bfloat16 [8192, 2048], P('col', 'row')
Outputs:
- root_inverse: float32 [8192, 8192], P('row', 'col')
- child_inverse: float32 [2048, 8192], P('col', 'row')
Inputs may be any that keep to these rules, and one draw needn't show every extreme that they name: sel_tiles holds 32 distinct tile indices in increasing order; rows of coupling outside the listed tiles are zero. factor is lower triangular with a diagonal between 1 and 1.5.
All inputs are finite; a program needn't handle non-finite values.
Results may differ from a plain program's by a relative error of at most 0.003.
Values may be sent and summed in bfloat16 or wider, within the bound.
A program may use at most 128 MiB of HBM per device.

v0:
```python
import jax
import jax.numpy as jnp
from jax import lax
from jax.sharding import PartitionSpec as P

TILE = 128


def from_root(value, axis, source):
    kept = jnp.where(lax.axis_index(axis) == source, value, 0).astype(value.dtype)
    return lax.psum(kept, axis)


def body(factor, sel_tiles, coupling):
    rows_here = factor.shape[0]
    row_index = lax.axis_index("row")
    whole = lax.all_gather(factor, "row", axis=0, tiled=True)
    ratio = lax.axis_size("row") // lax.axis_size("col")
    offset = row_index % ratio * rows_here
    piece = lax.dynamic_slice_in_dim(whole, offset, rows_here, 1)
    partner = from_root(piece, "col", row_index // ratio)
    gram = lax.dot_general(
        partner, whole, (((0,), (0,)), ((), ())), preferred_element_type=jnp.float32
    )
    coupling_full = lax.all_gather(coupling, "row", axis=1, tiled=True)
    rounded = gram.astype(jnp.bfloat16)
    global_rows = row_index * rows_here + jnp.arange(rows_here, dtype=jnp.int32)
    member = jnp.any((global_rows // TILE)[:, None] == sel_tiles[None, :], axis=1)
    summed = lax.psum_scatter(
        lax.dot_general(
            coupling_full, rounded, (((0,), (1,)), ((), ())), preferred_element_type=jnp.float32
        ),
        "col",
        scatter_dimension=0,
        tiled=True,
    )
    child = jnp.where(member[None, :], -summed, jnp.float32(0.0))
    return (gram, child)


def solution(mesh):
    placed = (P("row", "col"), P(), P("col", "row"))
    return jax.shard_map(
        body,
        mesh=mesh,
        in_specs=placed,
        out_specs=(P("row", "col"), P("col", "row")),
        check_vma=False,
    )
```

profile of v0, /device:TPU:0, one launch (start us, length us, event | category | flops | bytes accessed | tf_op | source)
XLA Modules:
  0.0 817.3 jit_solution(11417977400386051904)
XLA Ops:
  7.2 0.0 all-gather.3.cloned.1.call-start
  7.2 0.7 all-gather.3.cloned.1.call-update
  7.9 0.0 all-reduce.2.cloned.1.call-start
  8.0 293.0 %all-gather.3.cloned.1.call-done = bf16[8192,2048]{1,0:T(8,128)(2,1)} async-done(((bf16[1024,2048]{1,0:T(8,128)(2,1)}), bf16[8192,2048]{1,0:T(8,128)(2,1)}) %all-gather.3.cloned.1.call-update) | async-done | bytes 33554448 | tf_op jit(solution)/shard_map/all_gather | solution.py:17
  300.9 15.0 %dynamic-slice_select_fusion = bf16[8192,1024]{1,0:T(8,128)(2,1)} fusion(bf16[8192,2048]{1,0:T(8,128)(2,1)} %all-gather.3.cloned.1.call-done, s32[]{:T(128)S(6)} %select_n.38, pred[]{:T(512)S(6)} %eq.18), kind=kLoop, calls=%fused_computation | loop fusion | flops 8388608 | bytes 33554436 | tf_op jit(solution)/shard_map/jit(_where)/select_n | solution.py:10
  316.0 0.0 all-reduce.2.cloned.1.call-update
  316.0 0.0 all-gather.5.cloned.1.call-start
  316.0 0.7 all-gather.5.cloned.1.call-update
  316.7 0.0 reduce-scatter.2.cloned.1.call-start
  316.8 304.9 %all-reduce.2.cloned.1.call-done = bf16[8192,1024]{1,0:T(8,128)(2,1)} async-done(((bf16[8192,1024]{1,0:T(8,128)(2,1)}), bf16[8192,1024]{1,0:T(8,128)(2,1)}) %all-reduce.2.cloned.1.call-update) | async-done | bytes 16777232 | tf_op jit(solution)/shard_map/psum | solution.py:11
  621.7 43.9 %fusion.4 = f32[1024,2048]{1,0:T(8,128)} fusion(bf16[8192,1024]{1,0:T(8,128)(2,1)} %all-reduce.2.cloned.1.call-done, bf16[8192,2048]{1,0:T(8,128)(2,1)} %all-gather.3.cloned.1.call-done), kind=kOutput, calls=%fused_computation.14 | convolution fusion | flops 34359738368 | bytes 58720256 | tf_op jit(solution)/shard_map/dot_general | solution.py:22
  665.6 41.2 %all-gather.5.cloned.1.call-done = bf16[2048,2048]{1,0:T(8,128)(2,1)} async-done(((bf16[2048,256]{1,0:T(8,128)(2,1)}), bf16[2048,2048]{1,0:T(8,128)(2,1)}) %all-gather.5.cloned.1.call-update) | async-done | bytes 8388624 | tf_op jit(solution)/shard_map/all_gather | solution.py:25
  706.8 15.6 %convolution_bitcast_fusion = f32[2048,1024]{0,1:T(8,128)} fusion(bf16[2048,2048]{1,0:T(8,128)(2,1)} %all-gather.5.cloned.1.call-done, f32[1024,2048]{1,0:T(8,128)} %fusion.4), kind=kOutput, calls=%fused_computation.1 | convolution fusion | flops 8592031744 | bytes 25165824 | tf_op jit(solution)/shard_map/dot_general | solution.py:30
  722.4 0.0 copy-start
  722.4 0.0 reduce-scatter.2.cloned.1.call-update
  722.5 0.6 copy-done
  723.1 0.1 compare_reduce_fusion
  723.2 83.9 %reduce-scatter.2.cloned.1.call-done = f32[512,1024]{0,1:T(8,128)} async-done(((f32[2048,1024]{0,1:T(8,128)}), f32[512,1024]{0,1:T(8,128)}) %reduce-scatter.2.cloned.1.call-update) | async-done | bytes 2097168 | tf_op jit(solution)/shard_map/reduce_scatter | solution.py:29
  807.1 1.9 negate_select_fusion
  809.0 1.8 copy.6
  (1 shorter events, 0.0 us)
Async XLA Ops:
  7.2 293.8 %all-gather.3.cloned.1.call-start = ((), (), s32[]{:S(2)}) async-start(), calls=%async_computation.1 | async-start | bytes 37748736 | tf_op jit(solution)/shard_map/all_gather | solution.py:17
  7.9 613.8 %all-reduce.2.cloned.1.call-start = ((), (), s32[]{:S(2)}) async-start(), calls=%async_computation.2 | async-start | bytes 33554432 | tf_op jit(solution)/shard_map/psum | solution.py:11
  316.0 390.8 %all-gather.5.cloned.1.call-start = ((), (), s32[]{:S(2)}) async-start(), calls=%async_computation.3 | async-start | bytes 9437184 | tf_op jit(solution)/shard_map/all_gather | solution.py:25
  316.7 490.4 %reduce-scatter.2.cloned.1.call-start = ((), (), s32[]{:S(2)}) async-start(), calls=%async_computation.4 | async-start | bytes 10485760 | tf_op jit(solution)/shard_map/reduce_scatter | solution.py:29
  722.4 0.7 copy-start
Sparse Core Ops, SparseCore 0:
  9.6 291.3 all-gather.2
  316.1 305.5 all-reduce.1
  623.3 83.5 all-gather.4
  722.6 84.4 reduce-scatter.1
where the time goes:
time: 818 us; the launch traced here: 817 us
  waiting for transfers between devices  724 us (89%)
  matrix products  59.6 us (7%)
  other arithmetic  17 us (2%)
  between operations  13.8 us (2%)
    psum x1, waiting for transfers between devices, from_root(): return lax.psum(kept, axis)  305 us
    all_gather x1, waiting for transfers between devices, body(): whole = lax.all_gather(factor, 'row', axis=0, tiled=True)  293 us
    reduce_scatter x1, waiting for transfers between devices, body(): lax.psum_scatter(lax.dot_general(coupling_full, rounded, (((0,), (1,)), (...  83.9 us
    dot_general x1, matrix products, body(): lax.dot_general(partner, whole, (((0,), (0,)), ((), ())), preferred_eleme...  43.9 us
    all_gather x1, waiting for transfers between devices, body(): coupling_full = lax.all_gather(coupling, 'row', axis=1, tiled=True)  41.2 us
  transfers between devices with their start and end apart: 4, of which 4 were waited for; matrix products, arithmetic and copies ran while one was open for 5% of the time, Pallas kernels for 0%

commit v1 on v0

--- a/solution.py
+++ b/solution.py
@@ -12,6 +12,18 @@
 
 
 def body(factor, sel_tiles, coupling):
+
+    def arrange_quotas(local_values, array_axis):
+        many = lax.axis_size("row")
+        entries = tuple(((ix, (ix + 1) % many) for ix in range(many)))
+        q_next = [None] * many
+        q_next[many - 1] = local_values
+        for k0 in range(many - 2, -1, -1):
+            q_next[k0] = lax.ppermute(q_next[k0 + 1], perm=entries, axis_name="row")
+        left_arr = jnp.concatenate(q_next, axis=array_axis)
+        a_now = (lax.axis_index("row") + 1) * local_values.shape[array_axis]
+        return jnp.roll(left_arr, a_now, axis=array_axis)
+
     rows_here = factor.shape[0]
     row_index = lax.axis_index("row")
     whole = lax.all_gather(factor, "row", axis=0, tiled=True)
@@ -22,7 +34,7 @@
     gram = lax.dot_general(
         partner, whole, (((0,), (0,)), ((), ())), preferred_element_type=jnp.float32
     )
-    coupling_full = lax.all_gather(coupling, "row", axis=1, tiled=True)
+    coupling_full = arrange_quotas(coupling, 1)
     rounded = gram.astype(jnp.bfloat16)
     global_rows = row_index * rows_here + jnp.arange(rows_here, dtype=jnp.int32)
     member = jnp.any((global_rows // TILE)[:, None] == sel_tiles[None, :], axis=1)

time: 818 us -> 780 us (0.954)
  waiting for transfers between devices: 724 us -> 656 us
  local copies, waits for them, and re-layouts: 2.42 us -> 33.7 us
    psum x1, waiting for transfers between devices: 305 us -> 163 us  [from_root(): return lax.psum(kept, axis)]
    ppermute x0 -> x7, waiting for transfers between devices: none -> 112 us  [arrange_quotas(): q_next[k0] = lax.ppermute(q_next[k0 + 1], perm=entries, axis_name='row')]
    all_gather x1 -> x0, waiting for transfers between devices: 41.2 us -> none  [body(): coupling_full = lax.all_gather(coupling, 'row', axis=1, tiled=True)]
    unnamed x3 -> x33, local copies, waits for them, and re-layouts: 2.42 us -> 32.6 us
  transfers between devices with their start and end apart: 4 -> 10, of which waited for: 4 -> 10; matrix products, arithmetic and copies ran while one was open for 5% -> 3% of each run, Pallas kernels for 0% -> 0%
where the time goes in v1:
time: 780 us; the launch traced here: 779 us
  waiting for transfers between devices  656 us (84%)
  matrix products  56.5 us (7%)
  local copies, waits for them, and re-layouts  33.7 us (4%)
  other arithmetic  18.5 us (2%)
  between operations  13.8 us (2%)
    all_gather x1, waiting for transfers between devices, body(): whole = lax.all_gather(factor, 'row', axis=0, tiled=True)  293 us
    psum x1, waiting for transfers between devices, from_root(): return lax.psum(kept, axis)  163 us
    ppermute x7, waiting for transfers between devices, arrange_quotas(): q_next[k0] = lax.ppermute(q_next[k0 + 1], perm=entries, axis_name='row')  112 us
    reduce_scatter x1, waiting for transfers between devices, body(): lax.psum_scatter(lax.dot_general(coupling_full, rounded, (((0,), (1,)), (...  87.4 us
    dot_general x1, matrix products, body(): lax.dot_general(partner, whole, (((0,), (0,)), ((), ())), preferred_eleme...  43.1 us
    unnamed x33, local copies, waits for them, and re-layouts  32.6 us
  transfers between devices with their start and end apart: 10, of which 10 were waited for; matrix products, arithmetic and copies ran while one was open for 3% of the time, Pallas kernels for 0%

profile of v1, /device:TPU:0, one launch (start us, length us, event | category | flops | bytes accessed | tf_op | source)
XLA Modules:
  0.0 779.0 jit_solution(4246084666884449865)
XLA Ops:
  7.2 0.0 all-gather.2.cloned.1.call-start
  7.2 0.7 all-gather.2.cloned.1.call-update
  7.9 0.0 all-reduce.2.cloned.1.call-start
  8.0 293.0 %all-gather.2.cloned.1.call-done = bf16[8192,2048]{1,0:T(8,128)(2,1)} async-done(((bf16[1024,2048]{1,0:T(8,128)(2,1)}), bf16[8192,2048]{1,0:T(8,128)(2,1)}) %all-gather.2.cloned.1.call-update) | async-done | bytes 33554448 | tf_op jit(solution)/shard_map/all_gather | solution.py:29
  300.9 15.0 %dynamic-slice_select_fusion = bf16[8192,1024]{1,0:T(8,128)(2,1)} fusion(bf16[8192,2048]{1,0:T(8,128)(2,1)} %all-gather.2.cloned.1.call-done, s32[]{:T(128)S(6)} %select_n.50, pred[]{:T(512)S(6)} %eq.21), kind=kLoop, calls=%fused_computation | loop fusion | flops 8388608 | bytes 33554436 | tf_op jit(solution)/shard_map/jit(_where)/select_n | solution.py:10
  316.0 0.0 all-reduce.2.cloned.1.call-update
  316.0 0.0 reduce-scatter.2.cloned.1.call-start
  316.0 1.1 copy-done
  317.2 0.2 collective-permute-start
  317.4 15.8 %collective-permute-done = bf16[2048,256]{1,0:T(8,128)(2,1)S(1)} collective-permute-done((bf16[2048,256]{1,0:T(8,128)(2,1)S(1)}, bf16[2048,256]{1,0:T(8,128)(2,1)S(1)}, u32[]{:S(2)}, u32[]{:S(2)}) %collective-permute-start) | collective-permute-done | bytes 1048608 | tf_op jit(solution)/shard_map/ppermute | solution.py:22
  333.2 0.0 collective-permute-start.1
  333.2 16.0 %collective-permute-done.1 = bf16[2048,256]{1,0:T(8,128)(2,1)S(1)} collective-permute-done((bf16[2048,256]{1,0:T(8,128)(2,1)S(1)}, bf16[2048,256]{1,0:T(8,128)(2,1)S(1)}, u32[]{:S(2)}, u32[]{:S(2)}) %collective-permute-start.1) | collective-permute-done | bytes 1048608 | tf_op jit(solution)/shard_map/ppermute | solution.py:22
  349.2 16.0 %collective-permute-done.2 = bf16[2048,256]{1,0:T(8,128)(2,1)S(1)} collective-permute-done((bf16[2048,256]{1,0:T(8,128)(2,1)S(1)}, bf16[2048,256]{1,0:T(8,128)(2,1)S(1)}, u32[]{:S(2)}, u32[]{:S(2)}) %collective-permute-start.2) | collective-permute-done | bytes 1048608 | tf_op jit(solution)/shard_map/ppermute | solution.py:22
  365.3 1.0 copy-done.1
  366.2 0.0 collective-permute-start.3
  366.2 16.0 %collective-permute-done.3 = bf16[2048,256]{1,0:T(8,128)(2,1)S(1)} collective-permute-done((bf16[2048,256]{1,0:T(8,128)(2,1)S(1)}, bf16[2048,256]{1,0:T(8,128)(2,1)S(1)}, u32[]{:S(2)}, u32[]{:S(2)}) %collective-permute-start.3) | collective-permute-done | bytes 1048608 | tf_op jit(solution)/shard_map/ppermute | solution.py:22
  382.3 1.0 copy-done.3
  383.2 0.0 collective-permute-start.4
  383.2 16.0 %collective-permute-done.4 = bf16[2048,256]{1,0:T(8,128)(2,1)S(1)} collective-permute-done((bf16[2048,256]{1,0:T(8,128)(2,1)S(1)}, bf16[2048,256]{1,0:T(8,128)(2,1)S(1)}, u32[]{:S(2)}, u32[]{:S(2)}) %collective-permute-start.4) | collective-permute-done | bytes 1048608 | tf_op jit(solution)/shard_map/ppermute | solution.py:22
  399.3 1.0 copy-done.5
  400.2 0.0 collective-permute-start.5
  400.2 16.1 %collective-permute-done.5 = bf16[2048,256]{1,0:T(8,128)(2,1)} collective-permute-done((bf16[2048,256]{1,0:T(8,128)(2,1)S(1)}, bf16[2048,256]{1,0:T(8,128)(2,1)}, u32[]{:S(2)}, u32[]{:S(2)}) %collective-permute-start.5) | collective-permute-done | bytes 1048608 | tf_op jit(solution)/shard_map/ppermute | solution.py:22
  416.4 16.3 %collective-permute-done.6 = bf16[2048,256]{1,0:T(8,128)(2,1)} collective-permute-done((bf16[2048,256]{1,0:T(8,128)(2,1)}, bf16[2048,256]{1,0:T(8,128)(2,1)}, u32[]{:S(2)}, u32[]{:S(2)}) %collective-permute-start.6) | collective-permute-done | bytes 1048608 | tf_op jit(solution)/shard_map/ppermute | solution.py:22
  432.7 2.3 constant_dynamic-update-slice_fusion.15
  435.0 2.3 constant_dynamic-update-slice_fusion.14
  437.3 2.4 constant_dynamic-update-slice_fusion.13
  439.8 2.4 constant_dynamic-update-slice_fusion.12
  442.1 2.4 constant_dynamic-update-slice_fusion.11
  444.5 1.1 constant_dynamic-update-slice_fusion.10
  445.6 1.1 constant_dynamic-update-slice_fusion.9
  446.7 1.1 constant_dynamic-update-slice_fusion.8
  447.8 2.3 constant_dynamic-update-slice_fusion.7
  450.1 2.3 constant_dynamic-update-slice_fusion.6
  452.4 1.1 constant_dynamic-update-slice_fusion.5
  453.5 1.1 constant_dynamic-update-slice_fusion.4
  454.5 1.1 constant_dynamic-update-slice_fusion.3
  455.6 1.1 constant_dynamic-update-slice_fusion.2
  456.7 1.1 constant_dynamic-update-slice_fusion.1
  457.9 1.1 constant_dynamic-update-slice_fusion
  458.9 162.8 %all-reduce.2.cloned.1.call-done = bf16[8192,1024]{1,0:T(8,128)(2,1)} async-done(((bf16[8192,1024]{1,0:T(8,128)(2,1)}), bf16[8192,1024]{1,0:T(8,128)(2,1)}) %all-reduce.2.cloned.1.call-update) | async-done | bytes 16777232 | tf_op jit(solution)/shard_map/psum | solution.py:11
  621.7 43.1 %fusion.7 = f32[1024,2048]{1,0:T(8,128)S(1)} fusion(bf16[8192,1024]{1,0:T(8,128)(2,1)} %all-reduce.2.cloned.1.call-done, bf16[8192,2048]{1,0:T(8,128)(2,1)} %all-gather.2.cloned.1.call-done), kind=kOutput, calls=%fused_computation.32 | convolution fusion | flops 34359738368 | bytes 58720256 | tf_op jit(solution)/shard_map/dot_general | solution.py:34
  664.8 0.0 copy-start.8
  664.8 3.4 copy-done.8
  668.2 13.4 %fusion = f32[2048,1024]{1,0:T(8,128)} fusion(bf16[2048,4096]{1,0:T(8,128)(2,1)} %constant_dynamic-update-slice_fusion, s32[]{:T(128)S(6)} %select_n.54, f32[1024,2048]{1,0:T(8,128)S(1)} %fusion.7), kind=kOutput, calls=%fused_computation.1 | convolution fusion | flops 8592031744 | bytes 25165828 | tf_op jit(solution)/shard_map/dot_general | solution.py:42
  681.6 0.0 reduce-scatter.2.cloned.1.call-update
  681.7 0.1 compare_reduce_fusion
  681.8 87.4 %reduce-scatter.2.cloned.1.call-done = f32[512,1024]{1,0:T(8,128)} async-done(((f32[2048,1024]{1,0:T(8,128)}), f32[512,1024]{1,0:T(8,128)}) %reduce-scatter.2.cloned.1.call-update) | async-done | bytes 2097168 | tf_op jit(solution)/shard_map/reduce_scatter | solution.py:41
  769.1 3.3 negate_select_fusion
  (15 shorter events, 0.0 us)
Async XLA Ops:
  7.2 293.8 %all-gather.2.cloned.1.call-start = ((), (), s32[]{:S(2)}) async-start(), calls=%async_computation.1 | async-start | bytes 37748736 | tf_op jit(solution)/shard_map/all_gather | solution.py:29
  7.9 613.8 %all-reduce.2.cloned.1.call-start = ((), (), s32[]{:S(2)}) async-start(), calls=%async_computation.2 | async-start | bytes 33554432 | tf_op jit(solution)/shard_map/psum | solution.py:11
  316.0 1.2 copy-start
  316.0 453.1 %reduce-scatter.2.cloned.1.call-start = ((), (), s32[]{:S(2)}) async-start(), calls=%async_computation.3 | async-start | bytes 10485760 | tf_op jit(solution)/shard_map/reduce_scatter | solution.py:41
  317.2 16.0 %collective-permute-start = (bf16[2048,256]{1,0:T(8,128)(2,1)S(1)}, bf16[2048,256]{1,0:T(8,128)(2,1)S(1)}, u32[]{:S(2)}, u32[]{:S(2)}) collective-permute-start(bf16[2048,256]{1,0:T(8,128)(2,1)S(1)} %copy-done), channel_id=1, source_target_pairs={{0,4},{4,8},{8,12},{12,16},{16,20},{20,24},{24,28},{28,0},{1,5},{5... | collective-permute-start | bytes 3145736 | tf_op jit(solution)/shard_map/ppermute | solution.py:22
  333.2 16.0 %collective-permute-start.1 = (bf16[2048,256]{1,0:T(8,128)(2,1)S(1)}, bf16[2048,256]{1,0:T(8,128)(2,1)S(1)}, u32[]{:S(2)}, u32[]{:S(2)}) collective-permute-start(bf16[2048,256]{1,0:T(8,128)(2,1)S(1)} %collective-permute-done), channel_id=1, source_target_pairs={{0,4},{4,8},{8,12},{12,16},{16,20},{20,24},{24,28},{28,0},{1,5},{5... | collective-permute-start | bytes 3145736 | tf_op jit(solution)/shard_map/ppermute | solution.py:22
  349.2 16.0 %collective-permute-start.2 = (bf16[2048,256]{1,0:T(8,128)(2,1)S(1)}, bf16[2048,256]{1,0:T(8,128)(2,1)S(1)}, u32[]{:S(2)}, u32[]{:S(2)}) collective-permute-start(bf16[2048,256]{1,0:T(8,128)(2,1)S(1)} %collective-permute-done.1), channel_id=1, source_target_pairs={{0,4},{4,8},{8,12},{12,16},{16,20},{20,24},{24,28},{28,0},{1,5},{5... | collective-permute-start | bytes 3145736 | tf_op jit(solution)/shard_map/ppermute | solution.py:22
  365.3 1.0 copy-start.1
  366.2 16.0 %collective-permute-start.3 = (bf16[2048,256]{1,0:T(8,128)(2,1)S(1)}, bf16[2048,256]{1,0:T(8,128)(2,1)S(1)}, u32[]{:S(2)}, u32[]{:S(2)}) collective-permute-start(bf16[2048,256]{1,0:T(8,128)(2,1)S(1)} %collective-permute-done.2), channel_id=1, source_target_pairs={{0,4},{4,8},{8,12},{12,16},{16,20},{20,24},{24,28},{28,0},{1,5},{5... | collective-permute-start | bytes 3145736 | tf_op jit(solution)/shard_map/ppermute | solution.py:22
  382.3 1.0 copy-start.3
  383.2 16.0 %collective-permute-start.4 = (bf16[2048,256]{1,0:T(8,128)(2,1)S(1)}, bf16[2048,256]{1,0:T(8,128)(2,1)S(1)}, u32[]{:S(2)}, u32[]{:S(2)}) collective-permute-start(bf16[2048,256]{1,0:T(8,128)(2,1)S(1)} %collective-permute-done.3), channel_id=1, source_target_pairs={{0,4},{4,8},{8,12},{12,16},{16,20},{20,24},{24,28},{28,0},{1,5},{5... | collective-permute-start | bytes 3145736 | tf_op jit(solution)/shard_map/ppermute | solution.py:22
  399.3 1.0 copy-start.5
  400.2 16.1 %collective-permute-start.5 = (bf16[2048,256]{1,0:T(8,128)(2,1)S(1)}, bf16[2048,256]{1,0:T(8,128)(2,1)}, u32[]{:S(2)}, u32[]{:S(2)}) collective-permute-start(bf16[2048,256]{1,0:T(8,128)(2,1)S(1)} %collective-permute-done.4), channel_id=1, source_target_pairs={{0,4},{4,8},{8,12},{12,16},{16,20},{20,24},{24,28},{28,0},{1,5},{5... | collective-permute-start | bytes 3145736 | tf_op jit(solution)/shard_map/ppermute | solution.py:22
  416.4 16.3 %collective-permute-start.6 = (bf16[2048,256]{1,0:T(8,128)(2,1)}, bf16[2048,256]{1,0:T(8,128)(2,1)}, u32[]{:S(2)}, u32[]{:S(2)}) collective-permute-start(bf16[2048,256]{1,0:T(8,128)(2,1)} %collective-permute-done.5), channel_id=1, source_target_pairs={{0,4},{4,8},{8,12},{12,16},{16,20},{20,24},{24,28},{28,0},{1,5},{5... | collective-permute-start | bytes 3145736 | tf_op jit(solution)/shard_map/ppermute | solution.py:22
  416.4 36.0 %copy-start.6 = (bf16[2048,256]{1,0:T(8,128)(2,1)S(1)}, bf16[2048,256]{1,0:T(8,128)(2,1)}, u32[]{:S(2)}) copy-start(bf16[2048,256]{1,0:T(8,128)(2,1)} %copy-done.5) | copy-start | bytes 3145732
  416.4 37.1 %copy-start.4 = (bf16[2048,256]{1,0:T(8,128)(2,1)S(1)}, bf16[2048,256]{1,0:T(8,128)(2,1)}, u32[]{:S(2)}) copy-start(bf16[2048,256]{1,0:T(8,128)(2,1)} %copy-done.3) | copy-start | bytes 3145732
  416.4 38.2 %copy-start.2 = (bf16[2048,256]{1,0:T(8,128)(2,1)S(1)}, bf16[2048,256]{1,0:T(8,128)(2,1)}, u32[]{:S(2)}) copy-start(bf16[2048,256]{1,0:T(8,128)(2,1)} %copy-done.1) | copy-start | bytes 3145732
  664.8 3.4 copy-start.8
  668.2 13.5 %copy-start.7 = (s32[32]{0:T(128)S(1)}, s32[32]{0:T(128)}, u32[]{:S(2)}) copy-start(s32[32]{0:T(128)} %param.4) | copy-start | bytes 388
Sparse Core Ops, SparseCore 0:
  9.6 291.3 all-gather.1
  316.1 305.5 all-reduce.1
  681.8 87.3 reduce-scatter.1
